TPU v7x, 32 devices: a whole 2x2x4 slice. The times are simulated.
32 devices in a mesh: rows: 8 (over z, y), dp: 4 (over x, core).
Axes of the slice: x: 2, y: 2, z: 4, core: 2. Of those that a mesh axis runs over, the one named last changes fastest.
Arguments:
- weights: float32 [6144, 4096], P(('rows', 'dp'))
- moment: float32 [6144, 4096], P(('rows', 'dp'))
- second: float32 [6144, 4096], P(('rows', 'dp')), may hold values from 0.01 to 1
- tile_rows: bfloat16 [2048, 4096], P(('rows', 'dp')), may hold values from -6 to 6
- row_index: int32 [2048], P(('rows', 'dp')), may hold values from 0 to 191
- bucket_count: int32 [1024], P(('rows', 'dp')), may hold values from 1 to 2, as said below
Outputs:
- new_weights: float32 [6144, 4096], P(('rows', 'dp'))
- new_moment: float32 [6144, 4096], P(('rows', 'dp'))
- new_second: float32 [6144, 4096], P(('rows', 'dp'))
Inputs may be any that keep to these rules, and one draw needn't show every extreme that they name: `bucket_count`: at least one slot of every sender and owner is live; in every draw some owner receives 2 live slots from every sender. `row_index`: rows may repeat within and across senders.
All inputs are finite; a program needn't handle non-finite values.
Results may differ from a plain program's by a relative error of at most 0.0003.
Values may be sent and summed in bfloat16 or wider, within the bound.
A program may use at most 64 MiB of HBM per device.

v0:
```python
import jax
import jax.numpy as jnp
from jax import lax
from jax.sharding import PartitionSpec as P

beta_one = 0.9
beta_two = 0.999
epsilon = 1e-06
decay = 0.01
rate = 0.1


def local(weights, moment, second, tile_rows, row_index, bucket_count):
    owners = lax.axis_size(("rows", "dp"))
    rows_here = weights.shape[0]
    slot_total = row_index.shape[0]
    capacity = slot_total // owners
    is_live = lax.broadcasted_iota(jnp.int32, (owners, capacity), 1) < bucket_count[:, None]
    target = jnp.where(is_live.reshape(-1), row_index, -1)
    weight_part = jnp.sum(weights * weights)
    arrived, landing = (
        lax.all_to_all(tile_rows, ("rows", "dp"), split_axis=0, concat_axis=0, tiled=True),
        lax.all_to_all(target, ("rows", "dp"), split_axis=0, concat_axis=0, tiled=True),
    )
    picker = (
        landing[None, :] == lax.broadcasted_iota(jnp.int32, (rows_here, slot_total), 0)
    ).astype(jnp.bfloat16)
    gradient = jnp.dot(picker, arrived, preferred_element_type=jnp.float32)
    new_moment = beta_one * moment + (1.0 - beta_one) * gradient
    new_second = beta_two * second + (1.0 - beta_two) * gradient * gradient
    update = new_moment / (jnp.sqrt(new_second) + epsilon) + decay * weights
    update_part = jnp.sum(update * update)
    weight_sq, update_sq = lax.psum((weight_part, update_part), ("rows", "dp"))
    trust_ratio = jnp.sqrt(weight_sq) / jnp.sqrt(update_sq + 1e-06)
    new_weights = weights - rate * trust_ratio * update
    return (new_weights, new_moment, new_second)


def solution(mesh):
    placed = (
        P(("rows", "dp"), None),
        P(("rows", "dp"), None),
        P(("rows", "dp"), None),
        P(("rows", "dp"), None),
        P(("rows", "dp")),
        P(("rows", "dp")),
    )
    return jax.shard_map(
        local,
        mesh=mesh,
        in_specs=placed,
        out_specs=(P(("rows", "dp"), None), P(("rows", "dp"), None), P(("rows", "dp"), None)),
        check_vma=False,
    )
```

profile of v0, /device:TPU:0, one launch (start us, length us, event | category | flops | bytes accessed | tf_op | source)
XLA Modules:
  0.0 91.9 jit_solution(8254244321637544853)
XLA Ops:
  0.6 0.0 copy-start
  0.6 0.9 iota_compare_fusion.2
  1.5 0.1 lt.14
  1.6 0.7 broadcast_select_fusion
  2.3 0.7 all_to_all.14
  3.0 7.3 %all-to-all-start = ((s32[32,2,1]{1,2,0:T(1,128)}), s32[32,2,1]{1,2,0:T(1,128)S(1)}, u32[]{:S(2)}, u32[]{:S(2)}) async-start(s32[32,2,1]{1,2,0:T(1,128)} %bitcast), calls=%async_computation | async-start | bytes 32768 | tf_op jit(solution)/shard_map/all_to_all | solution.py:23
  10.3 2.2 %all_to_all.16 = bf16[32,2,4096]{2,1,0:T(2,128)(2,1)} reshape(bf16[64,4096]{1,0:T(8,128)(2,1)} %param.9) | data formatting | bytes 1048576 | tf_op jit(solution)/shard_map/all_to_all | solution.py:22
  12.5 4.9 %all-to-all-done = s32[32,2,1]{1,2,0:T(1,128)S(1)} async-done(((s32[32,2,1]{1,2,0:T(1,128)}), s32[32,2,1]{1,2,0:T(1,128)S(1)}, u32[]{:S(2)}, u32[]{:S(2)}) %all-to-all-start) | async-done | bytes 288 | tf_op jit(solution)/shard_map/all_to_all | solution.py:23
  17.4 3.3 %all-to-all-start.1 = ((bf16[32,2,4096]{2,1,0:T(2,128)(2,1)}), bf16[32,2,4096]{2,1,0:T(2,128)(2,1)}, u32[]{:S(2)}, u32[]{:S(2)}) async-start(bf16[32,2,4096]{2,1,0:T(2,128)(2,1)} %all_to_all.16), calls=%async_computation.1 | async-start | bytes 1048576 | tf_op jit(solution)/shard_map/all_to_all | solution.py:22
  20.8 0.5 broadcast.7
  21.3 0.7 reduce.3
  22.0 0.1 eq.10
  22.1 14.3 %all-to-all-done.1 = bf16[32,2,4096]{2,1,0:T(2,128)(2,1)} async-done(((bf16[32,2,4096]{2,1,0:T(2,128)(2,1)}), bf16[32,2,4096]{2,1,0:T(2,128)(2,1)}, u32[]{:S(2)}, u32[]{:S(2)}) %all-to-all-start.1) | async-done | bytes 524320 | tf_op jit(solution)/shard_map/all_to_all | solution.py:22
  36.4 2.0 %all_to_all.18 = bf16[64,4096]{1,0:T(8,128)(2,1)} reshape(bf16[32,2,4096]{2,1,0:T(2,128)(2,1)} %all-to-all-done.1) | data formatting | bytes 1048576 | tf_op jit(solution)/shard_map/all_to_all | solution.py:22
  38.4 0.0 copy-done
  38.4 7.0 %multiply_reduce_fusion = (f32[]{:T(128)}, f32[]{:T(128)}, f32[192,4096]{1,0:T(8,128)}, f32[192,4096]{1,0:T(8,128)}) fusion(f32[192,4096]{1,0:T(8,128)S(1)} %copy-done, f32[192,4096]{1,0:T(8,128)} %param.8, f32[192,4096]{1,0:T(8,128)} %param.7, bf16[64,4096]{1,0:T(8,128)(2,1)} %all_to_all.18, s32[64]{0:T(128)S(1)} %eq.10), kind=kOutput, calls=%fused_computation.3 | convolution fusion | flops 112472064 | bytes 16253192 | tf_op jit(solution)/shard_map/dot_general | solution.py:28
  45.4 39.1 %all-reduce = (f32[]{:T(128)}, f32[]{:T(128)}) all-reduce(f32[]{:T(128)} %get-tuple-element.4, f32[]{:T(128)} %get-tuple-element.3), channel_id=1, replica_groups=mesh['rows'=8,'dp'=4] {'rows','dp'}, use_global_device_ids=true, to_apply=%region_1.2 | all-reduce | flops 2 | bytes 16 | tf_op jit(solution)/shard_map/psum | solution.py:33
  85.9 6.0 %multiply_subtract_fusion = f32[192,4096]{1,0:T(8,128)} fusion(f32[192,4096]{1,0:T(8,128)S(1)} %copy-done, f32[]{:T(128)S(6)} %mul.61, f32[192,4096]{1,0:T(8,128)} %get-tuple-element.8, f32[192,4096]{1,0:T(8,128)} %get-tuple-element.7), kind=kLoop, calls=%fused_computation.2 | loop fusion | flops 4718592 | bytes 12582916 | tf_op jit(solution)/shard_map/sub | solution.py:35
Async XLA Ops:
  0.6 37.8 %copy-start = (f32[192,4096]{1,0:T(8,128)S(1)}, f32[192,4096]{1,0:T(8,128)}, u32[]{:S(2)}) copy-start(f32[192,4096]{1,0:T(8,128)} %param.6) | copy-start | bytes 9437188
  3.0 14.4 %all-to-all-start = ((s32[32,2,1]{1,2,0:T(1,128)}), s32[32,2,1]{1,2,0:T(1,128)S(1)}, u32[]{:S(2)}, u32[]{:S(2)}) async-start(s32[32,2,1]{1,2,0:T(1,128)} %bitcast), calls=%async_computation | async-start | bytes 32768 | tf_op jit(solution)/shard_map/all_to_all | solution.py:23
  17.4 18.9 %all-to-all-start.1 = ((bf16[32,2,4096]{2,1,0:T(2,128)(2,1)}), bf16[32,2,4096]{2,1,0:T(2,128)(2,1)}, u32[]{:S(2)}, u32[]{:S(2)}) async-start(bf16[32,2,4096]{2,1,0:T(2,128)(2,1)} %all_to_all.16), calls=%async_computation.1 | async-start | bytes 1048576 | tf_op jit(solution)/shard_map/all_to_all | solution.py:22
where the time goes:
time: 92.4 us; the launch traced here: 91.9 us
  blocking collectives  39.1 us (42%)
  waiting for transfers between devices  19.2 us (21%)
  starting transfers between devices  10.7 us (12%)
  other arithmetic  8.18 us (9%)
  matrix products  7.01 us (8%)
  local copies, waits for them, and re-layouts  5.65 us (6%)
  between operations  2.04 us (2%)
    psum x1, blocking collectives, local(): weight_sq, update_sq = lax.psum((weight_part, update_part), ('rows', 'dp'))  39.1 us
    all_to_all x1, waiting for transfers between devices, local(): lax.all_to_all(tile_rows, ('rows', 'dp'), split_axis=0, concat_axis=0, ti...  14.3 us
    all_to_all x1, starting transfers between devices, local(): lax.all_to_all(target, ('rows', 'dp'), split_axis=0, concat_axis=0, tiled...  7.33 us
    dot_general x1, matrix products, local(): gradient = jnp.dot(picker, arrived, preferred_element_type=jnp.float32)  7.01 us
    sub x1, other arithmetic, local(): new_weights = weights - rate * trust_ratio * update  5.96 us
    all_to_all x1, waiting for transfers between devices, local(): lax.all_to_all(target, ('rows', 'dp'), split_axis=0, concat_axis=0, tiled...  4.93 us
    all_to_all x2, local copies, waits for them, and re-layouts, local(): lax.all_to_all(tile_rows, ('rows', 'dp'), split_axis=0, concat_axis=0, ti...  4.2 us
    all_to_all x1, starting transfers between devices, local(): lax.all_to_all(tile_rows, ('rows', 'dp'), split_axis=0, concat_axis=0, ti...  3.33 us
  transfers between devices with their start and end apart: 2, of which 2 were waited for; matrix products, arithmetic and copies ran while one was open for 1% of the time, Pallas kernels for 0%

commit v1 on v0

v1 whole, which is shorter than its diff:
```python
import functools

import jax
import jax.numpy as jnp
from jax import lax
from jax.experimental import pallas as pl
from jax.experimental.pallas import tpu as pltpu
from jax.sharding import PartitionSpec as P

beta_one = 0.9
beta_two = 0.999
epsilon = 1e-06
decay = 0.01
rate = 0.1

AXES = ("rows", "dp")
LANES = 128
CHUNKS = 4


def exchange(
    n, fast, weights, moment, second, tiles, index, count,
    weight_out, moment_out, second_out, update_out, scale_out,
    staged, landed, index_all, count_all, parts, picker,
    load_sem, stage_sem, own_sem, tile_send, tile_recv, small_send, small_recv, part_send, part_recv,
):
    me = lax.axis_index("rows") * fast + lax.axis_index("dp")
    rows_here, width = weights.shape
    groups = width // LANES
    slots = index.shape[-1]
    capacity = slots // n
    per = groups // CHUNKS
    pack = tiles.shape[2]

    loads = [
        pltpu.make_async_copy(weights, weight_out, load_sem.at[0]),
        pltpu.make_async_copy(moment, moment_out, load_sem.at[1]),
        pltpu.make_async_copy(second, second_out, load_sem.at[2]),
    ]
    barrier = pltpu.get_barrier_semaphore()

    def place(device):
        return {"rows": device // fast, "dp": lax.rem(device, fast)}

    def peer_of(step):
        return lax.rem(me + 1 + lax.rem(step + n // 2 - 1, n - 1), n)

    @pl.loop(0, n - 1)
    def _(step):
        pl.semaphore_signal(
            barrier, inc=1, device_id=place(peer_of(step)),
            device_id_type=pl.DeviceIdType.MESH,
        )

    stage = [
        pltpu.make_async_copy(tiles, staged, stage_sem.at[0]),
        pltpu.make_async_copy(index, index_all.at[me], stage_sem.at[1]),
        pltpu.make_async_copy(count, count_all.at[me], stage_sem.at[2]),
    ]
    for copy in stage:
        copy.start()
    own = pltpu.make_async_copy(
        tiles.at[me // pack, :, lax.rem(me, pack)], landed.at[:, me], own_sem
    )
    own.start()
    for load in loads:
        load.start()
    for copy in stage:
        copy.wait()
    pl.semaphore_wait(barrier, n - 1)

    @pl.loop(0, n - 1)
    def _(step):
        peer = peer_of(step)
        for ref, k in ((index_all, 0), (count_all, 1)):
            pltpu.make_async_remote_copy(
                src_ref=ref.at[me], dst_ref=ref.at[me],
                send_sem=small_send.at[k], recv_sem=small_recv.at[k],
                device_id=place(peer), device_id_type=pl.DeviceIdType.MESH,
            ).start()

    for q in range(CHUNKS):
        span = pl.ds(q * per, per)

        @pl.loop(0, n - 1)
        def _(step):
            peer = peer_of(step)
            pltpu.make_async_remote_copy(
                src_ref=staged.at[peer // pack, span, lax.rem(peer, pack)],
                dst_ref=landed.at[span, me],
                send_sem=tile_send.at[q], recv_sem=tile_recv.at[q],
                device_id=place(peer), device_id_type=pl.DeviceIdType.MESH,
            ).start()

    loads[0].wait()

    def weight_step(g, total):
        w = weight_out[:, pl.ds(pl.multiple_of(g * LANES, LANES), LANES)]
        return total + jnp.sum((w * w).reshape(rows_here // 8, 8, LANES), axis=0)

    zero = jnp.zeros((8, LANES), jnp.float32)
    weight_sum = lax.fori_loop(0, groups, weight_step, zero, unroll=4)

    few = pl.ds(0, n - 1)
    for k, ref in enumerate((index_all, count_all)):
        pltpu.make_async_copy(ref.at[few], ref.at[few], small_recv.at[k]).wait()
    index_rows = index_all[:, 0, :]
    count_rows = count_all[:, 0, :]
    lane = lax.broadcasted_iota(jnp.int32, (n, slots), 1)
    sender = lax.broadcasted_iota(jnp.int32, (n, slots), 0)
    owner = lax.broadcasted_iota(jnp.int32, (n, n), 1)
    live = jnp.sum(jnp.where(owner == me, count_rows, 0), axis=1, keepdims=True)
    spread = jnp.zeros((n, slots), jnp.int32)
    for c in range(capacity):
        mine = jnp.sum(
            jnp.where(lane == me * capacity + c, index_rows, 0), axis=1, keepdims=True
        )
        mine = jnp.where(live > c, mine, -1)
        spread = spread + jnp.where(lane == sender * capacity + c, mine, 0)
    target = jnp.sum(spread, axis=0, keepdims=True)
    row = lax.broadcasted_iota(jnp.int32, (rows_here, slots), 0)
    picker[...] = jnp.where(row == target, 1.0, 0.0).astype(jnp.bfloat16)

    loads[1].wait()
    loads[2].wait()
    own.wait()
    update_sum = zero
    for q in range(CHUNKS):
        span = pl.ds(q * per, per)
        piece = landed.at[span, few]
        pltpu.make_async_copy(piece, piece, tile_recv.at[q]).wait()

        def step(g, total):
            cols = pl.ds(pl.multiple_of(g * LANES, LANES), LANES)
            block = landed[g].reshape(slots, LANES)
            gradient = jnp.dot(
                picker[...], block, preferred_element_type=jnp.float32
            )
            new_moment = beta_one * moment_out[:, cols] + (1.0 - beta_one) * gradient
            new_second = (
                beta_two * second_out[:, cols] + (1.0 - beta_two) * gradient * gradient
            )
            update = (
                new_moment / (jnp.sqrt(new_second) + epsilon)
                + decay * weight_out[:, cols]
            )
            moment_out[:, cols] = new_moment
            second_out[:, cols] = new_second
            update_out[:, cols] = update
            return total + jnp.sum(
                (update * update).reshape(rows_here // 8, 8, LANES), axis=0
            )

        update_sum = lax.fori_loop(q * per, (q + 1) * per, step, update_sum, unroll=4)

    parts[me, 0:1, :] = jnp.sum(weight_sum, axis=0, keepdims=True)
    parts[me, 1:2, :] = jnp.sum(update_sum, axis=0, keepdims=True)

    @pl.loop(0, n - 1)
    def _(step):
        pltpu.make_async_remote_copy(
            src_ref=parts.at[me], dst_ref=parts.at[me],
            send_sem=part_send, recv_sem=part_recv,
            device_id=place(peer_of(step)), device_id_type=pl.DeviceIdType.MESH,
        ).start()

    for k, ref in enumerate((index_all, count_all)):
        pltpu.make_async_copy(ref.at[few], ref.at[few], small_send.at[k]).wait()
    for q in range(CHUNKS):
        piece = landed.at[pl.ds(q * per, per), few]
        pltpu.make_async_copy(piece, piece, tile_send.at[q]).wait()
    pltpu.make_async_copy(parts.at[few], parts.at[few], part_recv).wait()
    pltpu.make_async_copy(parts.at[few], parts.at[few], part_send).wait()

    def total(k):
        lanes = jnp.sum(parts[:, k, :], axis=0, keepdims=True)
        return jnp.sum(lanes, axis=1, keepdims=True)

    trust = jnp.sqrt(total(0)) / jnp.sqrt(total(1) + 1e-06)
    scale_out[...] = jnp.broadcast_to(rate * trust, scale_out.shape)


def finish(
    weight, moment, second, update, scale,
    weight_out, moment_out, second_out, fresh, sem, piece_sem,
):
    copies = [
        pltpu.make_async_copy(moment, moment_out, sem.at[0]),
        pltpu.make_async_copy(second, second_out, sem.at[1]),
    ]
    for copy in copies:
        copy.start()
    rows_here = weight.shape[0]
    pieces = piece_sem.shape[0]
    height = rows_here // pieces
    factor = scale[0:1, 0:1]
    out = []
    for p in range(pieces):
        span = pl.ds(p * height, height)
        fresh[span, :] = weight[span, :] - factor * update[span, :]
        copy = pltpu.make_async_copy(
            fresh.at[span], weight_out.at[span], piece_sem.at[p]
        )
        copy.start()
        out.append(copy)
    for copy in copies + out:
        copy.wait()


def local(n, fast, weights, moment, second, tile_rows, row_index, bucket_count):
    rows_here, width = weights.shape
    slots = row_index.shape[0]
    capacity = slots // n
    groups = width // LANES
    pack = 8 // capacity
    tiles = tile_rows.reshape(n // pack, pack, capacity, groups, LANES)
    tiles = tiles.transpose(0, 3, 1, 2, 4)
    table = (rows_here, width)
    anywhere = pl.BlockSpec(memory_space=pl.ANY)
    outside = pl.BlockSpec(memory_space=pltpu.HBM)
    inside = pl.BlockSpec(memory_space=pltpu.VMEM)
    f32 = jnp.float32
    held = pltpu.VMEM(table, f32)
    weight_v, moment_v, second_v, update_v, scale = pl.pallas_call(
        functools.partial(exchange, n, fast),
        out_shape=[jax.ShapeDtypeStruct(table, f32)] * 4
        + [jax.ShapeDtypeStruct((8, LANES), f32)],
        in_specs=[outside] * 6,
        out_specs=[inside] * 5,
        scratch_shapes=[
            pltpu.VMEM(tiles.shape, jnp.bfloat16),
            pltpu.VMEM((groups, n, capacity, LANES), jnp.bfloat16),
            pltpu.VMEM((n, 1, slots), jnp.int32),
            pltpu.VMEM((n, 1, n), jnp.int32),
            pltpu.VMEM((n, 2, LANES), f32),
            pltpu.VMEM((rows_here, slots), jnp.bfloat16),
            pltpu.SemaphoreType.DMA((3,)),
            pltpu.SemaphoreType.DMA((3,)),
            pltpu.SemaphoreType.DMA,
            pltpu.SemaphoreType.DMA((CHUNKS,)),
            pltpu.SemaphoreType.DMA((CHUNKS,)),
            pltpu.SemaphoreType.DMA((2,)),
            pltpu.SemaphoreType.DMA((2,)),
            pltpu.SemaphoreType.DMA,
            pltpu.SemaphoreType.DMA,
        ],
        compiler_params=pltpu.CompilerParams(
            collective_id=0, has_side_effects=True, vmem_limit_bytes=24 * 1024 * 1024
        ),
        name="exchange",
    )(*(
        pltpu.with_memory_space_constraint(x, pltpu.HBM)
        for x in (
            weights, moment, second, tiles,
            row_index.reshape(1, slots), bucket_count.reshape(1, n),
        )
    ))
    pieces = 6
    return tuple(pl.pallas_call(
        finish,
        out_shape=[jax.ShapeDtypeStruct(table, f32)] * 3,
        in_specs=[inside] * 5,
        out_specs=[anywhere] * 3,
        scratch_shapes=[
            held,
            pltpu.SemaphoreType.DMA((2,)),
            pltpu.SemaphoreType.DMA((pieces,)),
        ],
        compiler_params=pltpu.CompilerParams(vmem_limit_bytes=24 * 1024 * 1024),
        name="finish",
    )(weight_v, moment_v, second_v, update_v, scale))


def solution(mesh):
    n = mesh.shape["rows"] * mesh.shape["dp"]
    rows, flat = P(AXES, None), P(AXES)
    return jax.shard_map(
        functools.partial(local, n, mesh.shape["dp"]),
        mesh=mesh,
        in_specs=(rows, rows, rows, rows, flat, flat),
        out_specs=(rows, rows, rows),
        check_vma=False,
    )
```

time: 92.4 us -> 32.8 us (0.35)
  blocking collectives: 39.1 us -> 0 us
  Pallas kernels: 0 us -> 32 us
  waiting for transfers between devices: 19.2 us -> 0 us
  starting transfers between devices: 10.7 us -> 0 us
  other arithmetic: 8.18 us -> 0 us
  matrix products: 7.01 us -> 0 us
  local copies, waits for them, and re-layouts: 5.65 us -> 0 us
  between operations: 2.04 us -> 0.64 us
    psum x1 -> x0, blocking collectives: 39.1 us -> none  [local(): weight_sq, update_sq = lax.psum((weight_part, update_part), ('rows', 'dp'))]
    pallas_call x0 -> x2, Pallas kernels: none -> 32 us  [the longest x1 28.3 us: local(): pl.pallas_call(functools.partial(exchange, n, fast), out_shape=[jax.Shape...]
    all_to_all x2 -> x0, waiting for transfers between devices: 19.2 us -> none  [the longest x1 14.3 us: local(): lax.all_to_all(tile_rows, ('rows', 'dp'), split_axis=0, concat_axis=0, ti...]
    all_to_all x2 -> x0, starting transfers between devices: 10.7 us -> none  [the longest x1 7.33 us: local(): lax.all_to_all(target, ('rows', 'dp'), split_axis=0, concat_axis=0, tiled...]
    dot_general x1 -> x0, matrix products: 7.01 us -> none  [local(): gradient = jnp.dot(picker, arrived, preferred_element_type=jnp.float32)]
    sub x1 -> x0, other arithmetic: 5.96 us -> none  [local(): new_weights = weights - rate * trust_ratio * update]
    all_to_all x4 -> x0, local copies, waits for them, and re-layouts: 5.43 us -> none  [the longest x2 4.2 us: local(): lax.all_to_all(tile_rows, ('rows', 'dp'), split_axis=0, concat_axis=0, ti...]
  transfers between devices with their start and end apart: 2 -> 0, of which waited for: 2 -> 0; matrix products, arithmetic and copies ran while one was open for 1% -> 0% of each run, Pallas kernels for 0% -> 0%
where the time goes in v1:
time: 32.8 us; the launch traced here: 32.7 us
  Pallas kernels  32 us (98%)
  between operations  0.64 us (2%)
    pallas_call x1, Pallas kernels, local(): pl.pallas_call(functools.partial(exchange, n, fast), out_shape=[jax.Shape...  28.3 us
    pallas_call x1, Pallas kernels, local(): pl.pallas_call(finish, out_shape=[jax.ShapeDtypeStruct(table, f32)] * 3,...  3.73 us

profile of v1, /device:TPU:0, one launch (start us, length us, event | category | flops | bytes accessed | tf_op | source)
XLA Modules:
  0.0 32.7 jit_solution(14989271947594515824)
XLA Ops:
  0.6 28.3 %exchange.1 = (f32[192,4096]{1,0:T(8,128)S(1)}, f32[192,4096]{1,0:T(8,128)S(1)}, f32[192,4096]{1,0:T(8,128)S(1)}, f32[192,4096]{1,0:T(8,128)S(1)}, f32[8,128]{1,0:T(8,128)S(1)}) custom-call(f32[192,4096]{1,0:T(8,128)} %weights.1, f32[192,4096]{1,0:T(8,128)} %moment.1, f32[192,4096]{1,0:T(8,128)} %second.1, bf16[8,32,4,2,128]{4,3,2,1,0:T(2,128)(2,1)} %bitcast.5, ...), custom_call_target="tpu_custom_call" | custom-call | tf_op jit(solution)/shard_map/exchange/pallas_call | solution.py:224
  28.9 3.7 %finish.1 = (f32[192,4096]{1,0:T(8,128)}, f32[192,4096]{1,0:T(8,128)}, f32[192,4096]{1,0:T(8,128)}) custom-call(f32[192,4096]{1,0:T(8,128)S(1)} %get-tuple-element.8.weight, f32[192,4096]{1,0:T(8,128)S(1)} %get-tuple-element.9.moment, f32[192,4096]{1,0:T(8,128)S(1)} %get-tuple-element.10.second, f32[192,4096]{1,0:T(8,128)S(1)} %get-tuple-element.11.update, ...), custom_call_target="tpu_custom_call" | custom-call | tf_op jit(solution)/shard_map/finish/pallas_call | solution.py:259

commit v2 on v1

--- a/solution.py
+++ b/solution.py
@@ -15,7 +15,7 @@
 
 AXES = ("rows", "dp")
 LANES = 128
-CHUNKS = 4
+CHUNKS = 8
 
 
 def exchange(
@@ -43,7 +43,7 @@
         return {"rows": device // fast, "dp": lax.rem(device, fast)}
 
     def peer_of(step):
-        return lax.rem(me + 1 + lax.rem(step + n // 2 - 1, n - 1), n)
+        return lax.rem(me + 1 + step, n)
 
     @pl.loop(0, n - 1)
     def _(step):
@@ -69,16 +69,6 @@
         copy.wait()
     pl.semaphore_wait(barrier, n - 1)
 
-    @pl.loop(0, n - 1)
-    def _(step):
-        peer = peer_of(step)
-        for ref, k in ((index_all, 0), (count_all, 1)):
-            pltpu.make_async_remote_copy(
-                src_ref=ref.at[me], dst_ref=ref.at[me],
-                send_sem=small_send.at[k], recv_sem=small_recv.at[k],
-                device_id=place(peer), device_id_type=pl.DeviceIdType.MESH,
-            ).start()
-
     for q in range(CHUNKS):
         span = pl.ds(q * per, per)
 
@@ -91,6 +81,18 @@
                 send_sem=tile_send.at[q], recv_sem=tile_recv.at[q],
                 device_id=place(peer), device_id_type=pl.DeviceIdType.MESH,
             ).start()
+
+        if q == 0:
+
+            @pl.loop(0, n - 1)
+            def _(step):
+                peer = peer_of(step)
+                for ref, k in ((index_all, 0), (count_all, 1)):
+                    pltpu.make_async_remote_copy(
+                        src_ref=ref.at[me], dst_ref=ref.at[me],
+                        send_sem=small_send.at[k], recv_sem=small_recv.at[k],
+                        device_id=place(peer), device_id_type=pl.DeviceIdType.MESH,
+                    ).start()
 
     loads[0].wait()
 

time: 32.8 us -> 31.7 us (0.966)
  Pallas kernels: 32 us -> 30.9 us
    pallas_call x1, Pallas kernels: 28.3 us -> 27.2 us  [local(): pl.pallas_call(functools.partial(exchange, n, fast), out_shape=[jax.Shape...]
where the time goes in v2:
time: 31.7 us; the launch traced here: 31.6 us
  Pallas kernels  30.9 us (97%)
  between operations  0.64 us (2%)
    pallas_call x1, Pallas kernels, local(): pl.pallas_call(functools.partial(exchange, n, fast), out_shape=[jax.Shape...  27.2 us
    pallas_call x1, Pallas kernels, local(): pl.pallas_call(finish, out_shape=[jax.ShapeDtypeStruct(table, f32)] * 3,...  3.73 us

profile of v2, /device:TPU:0, one launch (start us, length us, event | category | flops | bytes accessed | tf_op | source)
XLA Modules:
  0.0 31.6 jit_solution(10642764146603261687)
XLA Ops:
  0.6 27.2 %exchange.1 = (f32[192,4096]{1,0:T(8,128)S(1)}, f32[192,4096]{1,0:T(8,128)S(1)}, f32[192,4096]{1,0:T(8,128)S(1)}, f32[192,4096]{1,0:T(8,128)S(1)}, f32[8,128]{1,0:T(8,128)S(1)}) custom-call(f32[192,4096]{1,0:T(8,128)} %weights.1, f32[192,4096]{1,0:T(8,128)} %moment.1, f32[192,4096]{1,0:T(8,128)} %second.1, bf16[8,32,4,2,128]{4,3,2,1,0:T(2,128)(2,1)} %bitcast.5, ...), custom_call_target="tpu_custom_call" | custom-call | tf_op jit(solution)/shard_map/exchange/pallas_call | solution.py:226
  27.9 3.7 %finish.1 = (f32[192,4096]{1,0:T(8,128)}, f32[192,4096]{1,0:T(8,128)}, f32[192,4096]{1,0:T(8,128)}) custom-call(f32[192,4096]{1,0:T(8,128)S(1)} %get-tuple-element.8.weight, f32[192,4096]{1,0:T(8,128)S(1)} %get-tuple-element.9.moment, f32[192,4096]{1,0:T(8,128)S(1)} %get-tuple-element.10.second, f32[192,4096]{1,0:T(8,128)S(1)} %get-tuple-element.11.update, ...), custom_call_target="tpu_custom_call" | custom-call | tf_op jit(solution)/shard_map/finish/pallas_call | solution.py:261
